TPU v7x, 32 devices: a whole 2x2x4 slice. The times are simulated.
32 devices in a mesh: grp: 8 (over y, x, core), tile: 4 (over z).
Axes of the slice: x: 2, y: 2, z: 4, core: 2. Of those that a mesh axis runs over, the one named last changes fastest.
Arguments:
- atm_flux: float32 [6, 32768], P(None, ('grp', 'tile')), may hold values from -6 to 6
- send_block: int32 [32, 4, 4], P(('grp', 'tile')), may hold values from 0 to 7
- send_count: int32 [32, 4], P(('grp', 'tile')), may hold values from 1 to 4, as said below
- recv_block: int32 [32, 4, 4], P(('grp', 'tile')), may hold values from 0 to 63
- recv_weight: bfloat16 [32, 4, 4, 128, 128], P(('grp', 'tile')), may hold values from -0.5 to 0.5
- sea_temp: float32 [256, 1024], P('grp', 'tile'), may hold values from -6 to 6
- ocean_mask: int32 [256, 1024], P('grp', 'tile'), may hold values 0 or 1
Outputs:
- heat_flux: float32 [256, 1024], P('grp', 'tile')
- stress_curl: float32 [256, 1024], P('grp', 'tile')
- atm_return: float32 [4, 32768], P(None, ('grp', 'tile'))
Inputs may be any that keep to these rules, and one draw needn't show every extreme that they name: `send_count`: in every draw a quarter of the tile indices, drawn from the seed, receive exactly 4 blocks from every device of their group; every other pair carries 1 to 2 blocks.
All inputs are finite; a program needn't handle non-finite values. No bound on the sum of `ocean_mask` on one device may be relied on, other than what follows from the above.
Results may differ from a plain program's by a relative error of at most 0.0003.
Values sent between devices are 32-bit elements; how exact they have to be, the bound alone decides.
No kernel may reach another device: no remote copies, remote signals or barrier semaphores. Data moves between devices by JAX's collectives and lax.ppermute only.
A program may use at most 64 MiB of HBM per device.

v0:
```python
import jax
import jax.numpy as jnp
from jax import lax
from jax.sharding import PartitionSpec as P

precise = lax.Precision.HIGHEST


def extended(block, sides, width):
    for axis, dim in sides:
        count = lax.axis_size(axis)
        forward = [(i, i + 1) for i in range(count - 1)]
        forward.append((count - 1, 0))
        backward = [(target, source) for source, target in forward]
        low = lax.ppermute(
            lax.slice_in_dim(block, block.shape[dim] - width, None, axis=dim), axis, forward
        )
        high = lax.ppermute(lax.slice_in_dim(block, 0, width, axis=dim), axis, backward)
        block = jnp.concatenate([low, block, high], axis=dim)
    return block


def from_partner(value, axis, stride):
    return lax.ppermute(value, axis, [(i, i ^ 1 << stride) for i in range(lax.axis_size(axis))])


def bulk_formula(fields, surface_temp, ocean_mask):
    sea_share = ocean_mask.astype(jnp.float32)
    wind_u, wind_v, air_temp, air_vapor, short_down, long_down = [fields[k] for k in range(6)]
    wind_speed = jnp.sqrt(wind_u * wind_u + wind_v * wind_v + 0.5)
    stress_x = 0.8 * wind_speed * wind_u * sea_share
    stress_y = 0.8 * wind_speed * wind_v * sea_share
    sensible = 0.6 * wind_speed * (surface_temp - air_temp)
    latent = 0.7 * wind_speed * (jnp.exp(0.3 * surface_temp) - air_vapor)
    long_up = 0.4 * (1.0 + 0.2 * surface_temp) ** 4
    heat_flux = (0.94 * short_down + long_down - long_up - sensible - latent) * sea_share
    surface = jnp.stack([surface_temp, sensible, latent, long_up]) * sea_share[None]
    return (stress_x, stress_y, heat_flux, surface)


def per_device(atm_flux, send_block, send_count, recv_block, recv_weight, sea_temp, ocean_mask):
    tile_count = lax.axis_size("tile")
    field_count = atm_flux.shape[0]
    block_cells = recv_weight.shape[-1]
    slot_count = send_block.shape[2]
    atm_blocks = atm_flux.shape[1] // block_cells
    ocean_rows, ocean_cols = sea_temp.shape
    ocean_blocks = ocean_rows * ocean_cols // block_cells
    slot_range = jnp.arange(slot_count, dtype=jnp.int32)
    blocks = atm_flux.reshape(field_count, atm_blocks, block_cells)
    send_index = send_block[0]
    pair_count = send_count[0]
    live_slots = (slot_range[None, :] < pair_count[:, None]).astype(jnp.float32)
    chosen = jnp.take(blocks, send_index, axis=1) * live_slots[None, :, :, None]
    incoming = lax.all_to_all(chosen, "tile", split_axis=1, concat_axis=1, tiled=True)
    weight_wide = recv_weight[0].astype(jnp.float32)
    remapped = jnp.einsum("scij,fscj->fsci", weight_wide, incoming, precision=precise)
    dest_block = recv_block[0]
    onehot = (
        jnp.arange(ocean_blocks, dtype=jnp.int32)[:, None] == dest_block.reshape(-1)[None, :]
    ).astype(jnp.float32)
    landed = jnp.einsum(
        "ok,fkj->foj",
        onehot,
        remapped.reshape(field_count, tile_count * slot_count, block_cells),
        precision=precise,
    )
    fields = landed.reshape(field_count, ocean_rows, ocean_cols)
    stress_x, stress_y, heat_flux, surface = bulk_formula(fields, sea_temp, ocean_mask)
    sea_share = ocean_mask.astype(jnp.float32)
    padded = extended(jnp.stack([stress_x, stress_y]), (("grp", 1), ("tile", 2)), 1)
    mirror_row = stress_x[ocean_rows - 1]
    for bit_number in range(tile_count.bit_length() - 1):
        mirror_row = from_partner(mirror_row, "tile", bit_number)
    fold_values = -jnp.flip(mirror_row)
    group_index = lax.axis_index("grp")
    south_rim = jnp.where(group_index == 0, 0.0, padded[0, 0, 1:-1])
    north_rim = jnp.where(group_index == lax.axis_size("grp") - 1, fold_values, padded[0, -1, 1:-1])
    column_x = jnp.concatenate([south_rim[None], stress_x, north_rim[None]], axis=0)
    stress_curl = 0.5 * (padded[1, 1:-1, 2:] - padded[1, 1:-1, :-2]) - 0.5 * (
        column_x[2:] - column_x[:-2]
    )
    stress_curl = stress_curl * sea_share
    surface_blocks = surface.reshape(surface.shape[0], ocean_blocks, block_cells)
    chosen_back = jnp.take(surface_blocks, dest_block, axis=1)
    returned = jnp.einsum("scij,fsci->fscj", weight_wide, chosen_back, precision=precise)
    arrived = lax.all_to_all(returned, "tile", split_axis=1, concat_axis=1, tiled=True)
    arrived = arrived * live_slots[None, :, :, None]
    atm_onehot = (
        jnp.arange(atm_blocks, dtype=jnp.int32)[:, None] == send_index.reshape(-1)[None, :]
    ).astype(jnp.float32)
    atm_part = jnp.einsum(
        "ak,fkj->faj",
        atm_onehot,
        arrived.reshape(surface.shape[0], tile_count * slot_count, block_cells),
        precision=precise,
    )
    return (heat_flux, stress_curl, atm_part.reshape(surface.shape[0], atm_blocks * block_cells))


def solution(mesh):
    placed = (
        P(None, ("grp", "tile")),
        P(("grp", "tile"), None, None),
        P(("grp", "tile"), None),
        P(("grp", "tile"), None, None),
        P(("grp", "tile"), None, None, None, None),
        P("grp", "tile"),
        P("grp", "tile"),
    )
    return jax.shard_map(
        per_device,
        mesh=mesh,
        in_specs=placed,
        out_specs=(P("grp", "tile"), P("grp", "tile"), P(None, ("grp", "tile"))),
        check_vma=False,
    )
```

profile of v0, /device:TPU:0, one launch (start us, length us, event | category | flops | bytes accessed | tf_op | source)
XLA Modules:
  0.0 37.9 jit_solution(13872398486308174749)
XLA Ops:
  0.6 0.0 copy-start
  0.6 0.7 %compare_select_fusion.2 = s32[4,4,1]{1,0,2:T(4,128)S(1)} fusion(s32[1,4,4]{2,1,0:T(4,128)} %param.8), kind=kLoop, calls=%fused_computation.52 | loop fusion | flops 48 | bytes 128 | tf_op jit(solution)/shard_map/jit(_take)/jit(_where)/select_n | solution.py:54
  1.4 0.1 reshape.162
  1.5 0.0 copy-start.4
  1.5 0.0 copy-start.7
  1.5 0.7 %copy-done.4 = s32[1,4,4]{2,1,0:T(4,128)S(1)} copy-done((s32[1,4,4]{2,1,0:T(4,128)S(1)}, s32[1,4,4]{2,1,0:T(4,128)}, u32[]{:S(2)}) %copy-start.4) | copy-done | bytes 88
  2.2 0.0 copy-done.7
  2.2 0.1 fusion.25
  2.2 1.3 %gather_fusion = f32[16,6,128]{2,1,0:T(8,128)S(1)} fusion(f32[6,8,128]{2,0,1:T(8,128)} %bitcast.69, s32[1024]{0:T(1024)S(1)} %pad_clamp_fusion.1), kind=kCustom, calls=%fused_computation | custom fusion | bytes 98368 | tf_op jit(solution)/shard_map/jit(_take)/gather | solution.py:54
  3.6 0.7 %fusion.6 = f32[6,4,4,128]{3,2,0,1:T(4,128)} fusion(f32[4,4,6,128]{3,2,1,0:T(8,128)S(1)} %bitcast.65, f32[4,4]{1,0:T(4,128)S(1)} %get-tuple-element.21, pred[4,4]{1,0:T(4,128)(4,1)S(1)} %get-tuple-element.22), kind=kLoop, calls=%fused_computation.14 | loop fusion | flops 24576 | bytes 98384 | tf_op jit(solution)/shard_map/mul | solution.py:54
  4.3 0.0 copy-start.3
  4.3 0.0 copy-start.2
  4.3 6.5 %all-to-all-start = ((f32[6,4,4,128]{3,2,0,1:T(4,128)}), f32[6,4,4,128]{3,2,0,1:T(4,128)S(1)}, u32[]{:S(2)}, u32[]{:S(2)}) async-start(f32[6,4,4,128]{3,2,0,1:T(4,128)} %fusion.6), calls=%async_computation | async-start | bytes 98304 | tf_op jit(solution)/shard_map/all_to_all | solution.py:55
  10.7 0.0 copy-done.3
  10.7 0.1 eq.37
  10.8 0.1 eq.43
  10.9 0.0 copy-done.2
  10.9 0.0 copy-start.1
  11.0 0.7 %copy-done.1 = s32[32,256]{1,0:T(8,128)S(1)} copy-done((s32[32,256]{1,0:T(8,128)S(1)}, s32[32,256]{1,0:T(8,128)}, u32[]{:S(2)}) %copy-start.1) | copy-done | bytes 32792
  11.7 0.1 reshape.170
  11.8 4.7 %all-to-all-done = f32[6,4,4,128]{3,2,0,1:T(4,128)S(1)} async-done(((f32[6,4,4,128]{3,2,0,1:T(4,128)}), f32[6,4,4,128]{3,2,0,1:T(4,128)S(1)}, u32[]{:S(2)}, u32[]{:S(2)}) %all-to-all-start) | async-done | bytes 49184 | tf_op jit(solution)/shard_map/all_to_all | solution.py:55
  16.4 0.0 copy-done
  16.4 0.9 %fusion.1 = f32[4,4,6,128]{3,2,1,0:T(8,128)S(1)} fusion(bf16[1,4,4,128,128]{4,3,2,1,0:T(8,128)(2,1)S(1)} %copy-done, f32[6,4,4,128]{3,2,0,1:T(4,128)S(1)} %all-to-all-done), kind=kOutput, calls=%fused_computation.6 | convolution fusion | flops 18874368 | bytes 622592 | tf_op jit(solution)/shard_map/scij,fscj->fsci/dot_general | solution.py:57
  17.4 0.4 convolution_bitcast_fusion
  17.8 0.7 %multiply_bitcast_fusion = (f32[1,32,256]{2,1,0:T(8,128)S(1)}, f32[32,256]{1,0:T(8,128)S(1)}, f32[32,256]{1,0:T(8,128)}, f32[32,256]{1,0:T(8,128)S(1)}, f32[32,256]{1,0:T(8,128)S(1)}, /*index=5*/f32[32,256]{1,0:T(8,128)S(1)}) fusion(f32[32,256]{1,0:T(8,128)S(1)} %squeeze.40, s32[32,256]{1,0:T(8,128)S(1)} %copy-done.1, f32[32,256]{1,0:T(8,128)S(1)} %squeeze.39, ...), kind=kLoop, calls=%fused_computation.37 | loop fusion | flops 212992 | bytes 425984 | tf_op jit(solution)/shard_map/stack | solution.py:71
  18.5 0.1 collective-permute-start
  18.6 2.6 %collective-permute-start.1 = (f32[2,1,256]{2,1,0:T(1,128)S(1)}, f32[2,1,256]{2,1,0:T(1,128)S(1)}, u32[]{:S(2)}, u32[]{:S(2)}) collective-permute-start(f32[2,1,256]{2,1,0:T(1,128)S(1)} %get-tuple-element.18), channel_id=1, source_target_pairs={{4,0},{8,4},{12,8},{16,12},{20,16},{24,20},{28,24},{0,28},{5,1},{9... | collective-permute-start | bytes 6152 | tf_op jit(solution)/shard_map/ppermute | solution.py:18
  21.2 0.8 %collective-permute-start.4 = (f32[256]{0:T(256)S(1)}, f32[256]{0:T(256)S(1)}, u32[]{:S(2)}, u32[]{:S(2)}) collective-permute-start(f32[256]{0:T(256)S(1)} %bitcast.73), channel_id=1, source_target_pairs={{0,1},{1,0},{2,3},{3,2},{4,5},{5,4},{6,7},{7,6},{8,9},{9,8},{10,11... | collective-permute-start | bytes 3080 | tf_op jit(solution)/shard_map/ppermute | solution.py:24
  22.2 0.1 maximum_multiply_fusion
  22.3 0.6 %gather_fusion.1 = f32[16,4,128]{2,1,0:T(4,128)S(1)} fusion(f32[4,64,128]{2,0,1:T(4,128)S(1)} %maximum_multiply_fusion, s32[1024]{0:T(1024)S(1)} %pad_clamp_fusion), kind=kCustom, calls=%fused_computation.1 | custom fusion | bytes 65600 | tf_op jit(solution)/shard_map/jit(_take)/gather | solution.py:85
  22.9 1.2 %convolution_bitcast_fusion.1 = f32[4,4,4,128]{3,0,2,1:T(4,128)} fusion(bf16[1,4,4,128,128]{4,3,2,1,0:T(8,128)(2,1)S(1)} %copy-done, f32[4,4,4,128]{3,2,1,0:T(4,128)S(1)} %bitcast.68, pred[4,4]{1,0:T(4,128)(4,1)S(1)} %compare_and_fusion), kind=kOutput, calls=%fused_computation.3 | convolution fusion | flops 12591104 | bytes 589840 | tf_op jit(solution)/shard_map/scij,fsci->fscj/dot_general | solution.py:86
  24.1 3.3 %all-to-all-start.1 = ((f32[4,4,4,128]{3,0,2,1:T(4,128)}), f32[4,4,4,128]{3,0,2,1:T(4,128)S(1)}, u32[]{:S(2)}, u32[]{:S(2)}) async-start(f32[4,4,4,128]{3,0,2,1:T(4,128)} %convolution_bitcast_fusion.1), calls=%async_computation.1 | async-start | bytes 65536 | tf_op jit(solution)/shard_map/all_to_all | solution.py:87
  27.4 0.0 collective-permute-done.4
  27.4 2.9 %collective-permute-start.5 = (f32[256]{0:T(256)S(1)}, f32[256]{0:T(256)S(1)}, u32[]{:S(2)}, u32[]{:S(2)}) collective-permute-start(f32[256]{0:T(256)S(1)} %collective-permute-done.4), channel_id=1, source_target_pairs={{0,2},{1,3},{2,0},{3,1},{4,6},{5,7},{6,4},{7,5},{8,10},{9,11},{10,... | collective-permute-start | bytes 3080 | tf_op jit(solution)/shard_map/ppermute | solution.py:24
  30.3 0.0 collective-permute-done
  30.3 0.0 collective-permute-done.1
  30.3 0.0 copy-start.5
  30.3 0.1 fusion.29
  30.4 1.5 %collective-permute-start.3 = (f32[2,34,1]{2,1,0:T(8,128)S(1)}, f32[2,34,1]{2,1,0:T(8,128)S(1)}, u32[]{:S(2)}, u32[]{:S(2)}) collective-permute-start(f32[2,34,1]{2,1,0:T(8,128)S(1)} %get-tuple-element.17), channel_id=1, source_target_pairs={{0,1},{1,2},{2,3},{3,0},{4,5},{5,6},{6,7},{7,4},{8,9},{9,10},{10,1... | collective-permute-start | bytes 824 | tf_op jit(solution)/shard_map/ppermute | solution.py:15
  31.9 2.4 %collective-permute-start.2 = (f32[2,34,1]{2,1,0:T(8,128)S(1)}, f32[2,34,1]{2,1,0:T(8,128)S(1)}, u32[]{:S(2)}, u32[]{:S(2)}) collective-permute-start(f32[2,34,1]{2,1,0:T(8,128)S(1)} %get-tuple-element.16), channel_id=1, source_target_pairs={{1,0},{2,1},{3,2},{0,3},{5,4},{6,5},{7,6},{4,7},{9,8},{10,9},{11,1... | collective-permute-start | bytes 824 | tf_op jit(solution)/shard_map/ppermute | solution.py:18
  34.2 0.0 copy-done.5
  34.2 0.0 collective-permute-done.5
  34.2 0.1 rev.4
  34.3 0.0 slice-start
  34.3 0.7 %slice-done = f32[1,1,256]{2,1,0:T(1,128)S(1)} async-done(((f32[2,1,256]{2,1,0:T(1,128)}), f32[1,1,256]{2,1,0:T(1,128)S(1)}, s32[]{:S(2)}) %slice-start) | async-done | bytes 1048 | tf_op jit(solution)/shard_map/slice | solution.py:78
  35.0 0.0 copy-start.6
  35.0 1.3 %collective-permute-done.3 = f32[2,34,1]{2,1,0:T(8,128)S(1)} collective-permute-done((f32[2,34,1]{2,1,0:T(8,128)S(1)}, f32[2,34,1]{2,1,0:T(8,128)S(1)}, u32[]{:S(2)}, u32[]{:S(2)}) %collective-permute-start.3) | collective-permute-done | bytes 304 | tf_op jit(solution)/shard_map/ppermute | solution.py:15
  36.3 0.0 collective-permute-done.2
  36.3 0.0 copy-done.6
  36.3 0.7 %fusion.10 = f32[32,256]{1,0:T(8,128)} fusion(f32[32,256]{1,0:T(8,128)S(1)} %get-tuple-element.12, f32[1,256]{1,0:T(1,128)S(1)} %fusion.26, f32[1,256]{1,0:T(1,128)S(1)} %bitcast.72, f32[2,34,1]{2,1,0:T(8,128)S(1)} %collective-permute-done.3, f32[2,1,256]{2,1,0:T(1,128)S(1)} %copy-done.6, f32[2,1,256]{2,1,0:T(1,128)S(1)} %collective-permute-done, ...), kind=kLoop, calls=%fused_computation.19 | loop fusion | flops 139264 | bytes 170528 | tf_op jit(solution)/shard_map/mul | solution.py:83
  37.0 0.0 all-to-all-done.1
  37.0 0.1 broadcast_multiply_fusion
  37.1 0.1 convolution_bitcast_fusion.2
  37.2 0.6 %copy.32 = f32[1,4,8,128]{3,1,2,0:T(4,128)} copy(f32[1,4,8,128]{3,2,1,0:T(8,128)S(1)} %convolution_bitcast_fusion.2) | data formatting | bytes 32768
  (21 shorter events, 0.3 us)
Async XLA Ops:
  0.6 15.8 %copy-start = (bf16[1,4,4,128,128]{4,3,2,1,0:T(8,128)(2,1)S(1)}, bf16[1,4,4,128,128]{4,3,2,1,0:T(8,128)(2,1)}, u32[]{:S(2)}) copy-start(bf16[1,4,4,128,128]{4,3,2,1,0:T(8,128)(2,1)} %param.11) | copy-start | bytes 1572868
  1.5 0.7 %copy-start.4 = (s32[1,4,4]{2,1,0:T(4,128)S(1)}, s32[1,4,4]{2,1,0:T(4,128)}, u32[]{:S(2)}) copy-start(s32[1,4,4]{2,1,0:T(4,128)} %param.8) | copy-start | bytes 196
  1.5 0.7 %copy-start.7 = (s32[1,4]{1,0:T(1,128)S(1)}, s32[1,4]{1,0:T(1,128)}, u32[]{:S(2)}) copy-start(s32[1,4]{1,0:T(1,128)} %param.9) | copy-start | bytes 52
  4.3 6.5 %copy-start.3 = (s32[1,4,4]{2,1,0:T(4,128)S(1)}, s32[1,4,4]{2,1,0:T(4,128)}, u32[]{:S(2)}) copy-start(s32[1,4,4]{2,1,0:T(4,128)} %param.10) | copy-start | bytes 196
  4.3 6.7 %copy-start.2 = (f32[32,256]{1,0:T(8,128)S(1)}, f32[32,256]{1,0:T(8,128)}, u32[]{:S(2)}) copy-start(f32[32,256]{1,0:T(8,128)} %param.12) | copy-start | bytes 98308
  4.3 12.2 %all-to-all-start = ((f32[6,4,4,128]{3,2,0,1:T(4,128)}), f32[6,4,4,128]{3,2,0,1:T(4,128)S(1)}, u32[]{:S(2)}, u32[]{:S(2)}) async-start(f32[6,4,4,128]{3,2,0,1:T(4,128)} %fusion.6), calls=%async_computation | async-start | bytes 98304 | tf_op jit(solution)/shard_map/all_to_all | solution.py:55
  10.9 0.8 %copy-start.1 = (s32[32,256]{1,0:T(8,128)S(1)}, s32[32,256]{1,0:T(8,128)}, u32[]{:S(2)}) copy-start(s32[32,256]{1,0:T(8,128)} %param.13) | copy-start | bytes 98308
  18.5 11.7 %collective-permute-start = (f32[2,1,256]{2,1,0:T(1,128)S(1)}, f32[2,1,256]{2,1,0:T(1,128)S(1)}, u32[]{:S(2)}, u32[]{:S(2)}) collective-permute-start(f32[2,1,256]{2,1,0:T(1,128)S(1)} %get-tuple-element.19), channel_id=1, source_target_pairs={{0,4},{4,8},{8,12},{12,16},{16,20},{20,24},{24,28},{28,0},{1,5},{5... | collective-permute-start | bytes 6152 | tf_op jit(solution)/shard_map/ppermute | solution.py:15
  18.6 11.7 %collective-permute-start.1 = (f32[2,1,256]{2,1,0:T(1,128)S(1)}, f32[2,1,256]{2,1,0:T(1,128)S(1)}, u32[]{:S(2)}, u32[]{:S(2)}) collective-permute-start(f32[2,1,256]{2,1,0:T(1,128)S(1)} %get-tuple-element.18), channel_id=1, source_target_pairs={{4,0},{8,4},{12,8},{16,12},{20,16},{24,20},{28,24},{0,28},{5,1},{9... | collective-permute-start | bytes 6152 | tf_op jit(solution)/shard_map/ppermute | solution.py:18
  21.2 6.2 %collective-permute-start.4 = (f32[256]{0:T(256)S(1)}, f32[256]{0:T(256)S(1)}, u32[]{:S(2)}, u32[]{:S(2)}) collective-permute-start(f32[256]{0:T(256)S(1)} %bitcast.73), channel_id=1, source_target_pairs={{0,1},{1,0},{2,3},{3,2},{4,5},{5,4},{6,7},{7,6},{8,9},{9,8},{10,11... | collective-permute-start | bytes 3080 | tf_op jit(solution)/shard_map/ppermute | solution.py:24
  24.1 12.9 %all-to-all-start.1 = ((f32[4,4,4,128]{3,0,2,1:T(4,128)}), f32[4,4,4,128]{3,0,2,1:T(4,128)S(1)}, u32[]{:S(2)}, u32[]{:S(2)}) async-start(f32[4,4,4,128]{3,0,2,1:T(4,128)} %convolution_bitcast_fusion.1), calls=%async_computation.1 | async-start | bytes 65536 | tf_op jit(solution)/shard_map/all_to_all | solution.py:87
  27.4 6.8 %collective-permute-start.5 = (f32[256]{0:T(256)S(1)}, f32[256]{0:T(256)S(1)}, u32[]{:S(2)}, u32[]{:S(2)}) collective-permute-start(f32[256]{0:T(256)S(1)} %collective-permute-done.4), channel_id=1, source_target_pairs={{0,2},{1,3},{2,0},{3,1},{4,6},{5,7},{6,4},{7,5},{8,10},{9,11},{10,... | collective-permute-start | bytes 3080 | tf_op jit(solution)/shard_map/ppermute | solution.py:24
  30.3 3.9 %copy-start.5 = (f32[2,1,256]{2,1,0:T(1,128)}, f32[2,1,256]{2,1,0:T(1,128)S(1)}, u32[]{:S(2)}) copy-start(f32[2,1,256]{2,1,0:T(1,128)S(1)} %collective-permute-done.1) | copy-start | bytes 6148
  30.4 5.9 %collective-permute-start.3 = (f32[2,34,1]{2,1,0:T(8,128)S(1)}, f32[2,34,1]{2,1,0:T(8,128)S(1)}, u32[]{:S(2)}, u32[]{:S(2)}) collective-permute-start(f32[2,34,1]{2,1,0:T(8,128)S(1)} %get-tuple-element.17), channel_id=1, source_target_pairs={{0,1},{1,2},{2,3},{3,0},{4,5},{5,6},{6,7},{7,4},{8,9},{9,10},{10,1... | collective-permute-start | bytes 824 | tf_op jit(solution)/shard_map/ppermute | solution.py:15
  31.9 4.4 %collective-permute-start.2 = (f32[2,34,1]{2,1,0:T(8,128)S(1)}, f32[2,34,1]{2,1,0:T(8,128)S(1)}, u32[]{:S(2)}, u32[]{:S(2)}) collective-permute-start(f32[2,34,1]{2,1,0:T(8,128)S(1)} %get-tuple-element.16), channel_id=1, source_target_pairs={{1,0},{2,1},{3,2},{0,3},{5,4},{6,5},{7,6},{4,7},{9,8},{10,9},{11,1... | collective-permute-start | bytes 824 | tf_op jit(solution)/shard_map/ppermute | solution.py:18
  34.3 0.7 %slice-start = ((f32[2,1,256]{2,1,0:T(1,128)}), f32[1,1,256]{2,1,0:T(1,128)S(1)}, s32[]{:S(2)}) async-start(f32[2,1,256]{2,1,0:T(1,128)} %copy-done.5), calls=%async_computation.2 | async-start | bytes 2048 | tf_op jit(solution)/shard_map/slice | solution.py:78
  35.0 1.3 %copy-start.6 = (f32[2,1,256]{2,1,0:T(1,128)S(1)}, f32[2,1,256]{2,1,0:T(1,128)}, u32[]{:S(2)}) copy-start(f32[2,1,256]{2,1,0:T(1,128)} %copy-done.5) | copy-start | bytes 6148
where the time goes:
time: 38.4 us; the launch traced here: 37.9 us
  starting transfers between devices  20 us (52%)
  waiting for transfers between devices  5.95 us (15%)
  local copies, waits for them, and re-layouts  5.32 us (14%)
  other arithmetic  3.19 us (8%)
  matrix products  2.61 us (7%)
  between operations  0.82 us (2%)
    all_to_all x1, starting transfers between devices, per_device(): lax.all_to_all(chosen, 'tile', split_axis=1, concat_axis=1, tiled=True)  6.48 us
    ppermute x2, starting transfers between devices, extended(): lax.ppermute(lax.slice_in_dim(block, 0, width, axis=dim), axis, backward)  4.99 us
    all_to_all x1, waiting for transfers between devices, per_device(): lax.all_to_all(chosen, 'tile', split_axis=1, concat_axis=1, tiled=True)  4.65 us
    ppermute x2, starting transfers between devices, from_partner(): lax.ppermute(value, axis, [(i, i ^ 1 << stride) for i in range(lax.axis_s...  3.71 us
    all_to_all x1, starting transfers between devices, per_device(): lax.all_to_all(returned, 'tile', split_axis=1, concat_axis=1, tiled=True)  3.26 us
    unnamed x17, local copies, waits for them, and re-layouts  2.03 us
    ppermute x2, starting transfers between devices, extended(): lax.ppermute(lax.slice_in_dim(block, block.shape[dim] - width, None, axis...  1.53 us
    gather x1, local copies, waits for them, and re-layouts, per_device(): chosen = jnp.take(blocks, send_index, axis=1) * live_slots[None, :, :, None]  1.31 us
  transfers between devices with their start and end apart: 8, of which 2 were waited for; matrix products, arithmetic and copies ran while one was open for 9% of the time, Pallas kernels for 0%

commit v1 on v0

v1 whole, which is shorter than its diff:
```python
import functools

import jax
import jax.numpy as jnp
from jax import lax
from jax.experimental import pallas as pl
from jax.experimental.pallas import tpu as pltpu
from jax.sharding import PartitionSpec as P

SUB = 8
F32 = jnp.float32
BF16 = jnp.bfloat16
VMEM = pl.BlockSpec(memory_space=pltpu.VMEM)
SMEM = pl.BlockSpec(memory_space=pltpu.SMEM)
PARAMS = pltpu.CompilerParams(vmem_limit_bytes=4 * 1024 * 1024)


def round_up(value, unit):
    return -(-value // unit) * unit


def is_column_mask(mask):
    return mask > 0 and mask & (mask + 1) == 0


def pack_kernel(send_block, send_count, atm_flux, *outs):
    here = lax.axis_index("tile")
    field_count = atm_flux.shape[0]
    slot_count, rows, cells = outs[0].shape
    for mask, out in enumerate(outs):
        peer = here ^ mask
        count = send_count[0, peer]
        for slot in range(slot_count):
            start = pl.multiple_of(send_block[0, peer, slot] * cells, cells)
            chosen = atm_flux[:, pl.ds(start, cells)]
            out[slot, :field_count, :] = jnp.where(slot < count, chosen, 0.0)
            if rows > field_count:
                out[slot, field_count:, :] = jnp.zeros((rows - field_count, cells), F32)


def split(value):
    high = value.astype(BF16)
    low = (value - high.astype(F32)).astype(BF16)
    return high, low


def middle_kernel(tile_count, field_count, back_count, recv_block, weight, sea_temp, ocean_mask, *refs):
    arrived = refs[:tile_count]
    heat, stress_x, stress_y, even_row, odd_row = refs[tile_count : tile_count + 5]
    payload = refs[tile_count + 5 : 2 * tile_count + 5]
    landed, surface = refs[2 * tile_count + 5 :]
    here = lax.axis_index("tile")
    slot_count, field_rows, cells = arrived[0].shape
    rows, cols = sea_temp.shape
    halves = cols // cells
    tiles = rows // SUB
    pairs = [(mask, slot) for mask in range(tile_count) for slot in range(slot_count)]
    landed[...] = jnp.zeros_like(landed)
    for mask, slot in pairs:
        source = here ^ mask
        high, low = split(arrived[mask][slot])
        both = jnp.concatenate([high, low], axis=0)
        result = lax.dot_general(
            both, weight[0, source, slot], (((1,), (1,)), ((), ())), preferred_element_type=F32
        )
        start = pl.multiple_of(recv_block[0, source, slot] * field_rows, field_rows)
        landed[pl.ds(start, field_rows), :] += result[:field_rows] + result[field_rows:]
    surface_rows = surface.shape[0] // (rows * halves)
    lane = lax.broadcasted_iota(jnp.int32, (SUB, cells), 1)
    edge = jnp.zeros((SUB, cells), F32)
    for half in range(halves):
        span = slice(half * cells, (half + 1) * cells)
        fields = [
            landed[pl.ds(half * field_rows + k, rows, stride=halves * field_rows), :]
            for k in range(field_count)
        ]
        wind_u, wind_v, air_temp, air_vapor, short_down, long_down = fields
        temp = sea_temp[:, span]
        share = ocean_mask[:, span].astype(F32)
        speed = jnp.sqrt(wind_u * wind_u + wind_v * wind_v + 0.5)
        drag = 0.8 * speed * share
        along_x = drag * wind_u
        along_y = drag * wind_v
        sensible = 0.6 * speed * (temp - air_temp)
        latent = 0.7 * speed * (jnp.exp(0.3 * temp) - air_vapor)
        base = 1.0 + 0.2 * temp
        square = base * base
        long_up = 0.4 * (square * square)
        heat[:, span] = (0.94 * short_down + long_down - long_up - sensible - latent) * share
        stress_x[:, span] = along_x
        stress_y[:, span] = along_y
        even_row[half : half + 1, :] = along_x[rows - 1 :]
        odd_row[half : half + 1, :] = along_x[:1]
        for k, value in enumerate([temp, sensible, latent, long_up]):
            value = value * share
            high = value.astype(BF16).astype(F32)
            step = halves * surface_rows
            surface[pl.ds(half * surface_rows + k, rows, stride=step), :] = high
            surface[pl.ds(half * surface_rows + back_count + k, rows, stride=step), :] = value - high
        if half == 0:
            for q in range(tiles):
                part = along_y[q * SUB : (q + 1) * SUB]
                edge = jnp.where(lane == q, pltpu.roll(part, q, 1), edge)
        if half == halves - 1:
            for q in range(tiles):
                part = along_y[q * SUB : (q + 1) * SUB]
                moved = pltpu.roll(part, (tiles + q + 1) % cells, 1)
                edge = jnp.where(lane == tiles + q, moved, edge)
    back_rows = slot_count * back_count
    for mask in range(tile_count):
        if is_column_mask(mask):
            payload[mask][back_rows : back_rows + SUB, :] = edge
        if mask == tile_count - 1:
            payload[mask][back_rows + SUB : back_rows + SUB + halves, :] = even_row[...]
    odd = lax.axis_index("grp") % 2 == 1
    top, bottom = even_row[...], odd_row[...]
    even_row[...] = jnp.where(odd, bottom, top)
    odd_row[...] = jnp.where(odd, top, bottom)
    for mask, slot in pairs:
        source = here ^ mask
        start = pl.multiple_of(recv_block[0, source, slot] * surface_rows, surface_rows)
        chosen = surface[pl.ds(start, surface_rows), :].astype(BF16)
        result = jnp.dot(chosen, weight[0, source, slot], preferred_element_type=F32)
        payload[mask][slot * back_count : (slot + 1) * back_count, :] = (
            result[:back_count] + result[back_count : 2 * back_count]
        )


def final_kernel(tile_count, back_count, send_block, send_count, ocean_mask, stress_x, stress_y, near, far, *refs):
    payload = refs[:tile_count]
    curl, atm = refs[tile_count:]
    here = lax.axis_index("tile")
    group = lax.axis_index("grp")
    group_count = lax.axis_size("grp")
    rows, cols = stress_x.shape
    cells = payload[0].shape[1]
    slot_count = send_block.shape[2]
    back_rows = slot_count * back_count
    halves = cols // cells
    tiles = rows // SUB
    odd = group % 2 == 1
    south = jnp.where(odd, near[...], far[...])
    south = jnp.where(group == 0, 0.0, south)
    north = jnp.where(odd, far[...], near[...])
    fold = payload[tile_count - 1][back_rows + SUB : back_rows + SUB + halves, :]
    turn = cells - 1 - lax.broadcasted_iota(jnp.int32, (SUB, cells), 1)
    last = group == group_count - 1
    east_edge = jnp.zeros((SUB, cells), F32)
    west_edge = jnp.zeros((SUB, cells), F32)
    east_mask = here ^ ((here + 1) % tile_count)
    west_mask = here ^ ((here + tile_count - 1) % tile_count)
    for mask in range(tile_count):
        if is_column_mask(mask):
            value = payload[mask][back_rows : back_rows + SUB, :]
            east_edge = jnp.where(east_mask == mask, value, east_edge)
            west_edge = jnp.where(west_mask == mask, value, west_edge)
    east_halo = jnp.concatenate([pltpu.roll(east_edge, cells - 1 - q, 1) for q in range(tiles)], axis=0)
    west_halo = jnp.concatenate([pltpu.roll(west_edge, cells - tiles - q, 1) for q in range(tiles)], axis=0)
    lane = lax.broadcasted_iota(jnp.int32, (rows, cells), 1)
    row = lax.broadcasted_iota(jnp.int32, (rows, cells), 0)
    parts = [stress_y[:, half * cells : (half + 1) * cells] for half in range(halves)]
    ahead = [pltpu.roll(part, cells - 1, 1) for part in parts] + [east_halo]
    behind = [west_halo] + [pltpu.roll(part, 1, 1) for part in parts]
    for half in range(halves):
        span = slice(half * cells, (half + 1) * cells)
        mirrored = jnp.broadcast_to(fold[halves - 1 - half][None], (SUB, cells))
        mirrored = jnp.take_along_axis(mirrored, turn, axis=1)[:1]
        above = jnp.where(last, -mirrored, north[half][None])
        below = south[half][None]
        east = jnp.where(lane == cells - 1, ahead[half + 1], ahead[half])
        west = jnp.where(lane == 0, behind[half], behind[half + 1])
        part = stress_x[:, span]
        up = jnp.where(row == rows - 1, above, pltpu.roll(part, rows - 1, 0))
        down = jnp.where(row == 0, below, pltpu.roll(part, 1, 0))
        share = ocean_mask[:, span].astype(F32)
        curl[:, span] = (0.5 * (east - west) - 0.5 * (up - down)) * share
    atm[...] = jnp.zeros_like(atm)
    for mask in range(tile_count):
        peer = here ^ mask
        count = send_count[0, peer]
        for slot in range(slot_count):
            start = pl.multiple_of(send_block[0, peer, slot] * cells, cells)
            value = payload[mask][slot * back_count : (slot + 1) * back_count, :]
            atm[:, pl.ds(start, cells)] += jnp.where(slot < count, value, 0.0)


def per_device(atm_flux, send_block, send_count, recv_block, recv_weight, sea_temp, ocean_mask):
    tile_count = lax.axis_size("tile")
    group_count = lax.axis_size("grp")
    field_count = atm_flux.shape[0]
    slot_count = send_block.shape[2]
    cells = recv_weight.shape[-1]
    rows, cols = sea_temp.shape
    halves = cols // cells
    back_count = 4
    field_rows = round_up(field_count, SUB)
    surface_rows = round_up(2 * back_count, SUB)
    back_rows = slot_count * back_count
    shape = jax.ShapeDtypeStruct

    def swap(value, mask):
        return lax.ppermute(value, "tile", [(i, i ^ mask) for i in range(tile_count)])

    packed = pl.pallas_call(
        pack_kernel,
        out_shape=[shape((slot_count, field_rows, cells), F32)] * tile_count,
        in_specs=[SMEM, SMEM, VMEM],
        out_specs=[VMEM] * tile_count,
        compiler_params=PARAMS,
        name="pack",
    )(send_block, send_count, atm_flux)
    arrived = list(packed)
    for mask in reversed(range(1, tile_count)):
        arrived[mask] = swap(packed[mask], mask)

    def payload_rows(mask):
        extra = SUB if is_column_mask(mask) else 0
        return back_rows + extra + (halves if mask == tile_count - 1 else 0)

    outs = pl.pallas_call(
        functools.partial(middle_kernel, tile_count, field_count, back_count),
        out_shape=[shape((rows, cols), F32)] * 3
        + [shape((halves, cells), F32)] * 2
        + [shape((payload_rows(mask), cells), F32) for mask in range(tile_count)],
        in_specs=[SMEM] + [VMEM] * (3 + tile_count),
        out_specs=[VMEM] * (5 + tile_count),
        scratch_shapes=[
            pltpu.VMEM((rows * halves * field_rows, cells), F32),
            pltpu.VMEM((rows * halves * surface_rows, cells), F32),
        ],
        compiler_params=PARAMS,
        name="middle",
    )(recv_block, recv_weight, sea_temp, ocean_mask, *arrived)
    heat, stress_x, stress_y, near, far = outs[:5]
    payload = list(outs[5:])
    far = lax.ppermute(
        far, "grp", [(i, i + 1 if i % 2 else i - 1) for i in range(1, group_count - 1)]
    )
    for mask in reversed(range(1, tile_count)):
        payload[mask] = swap(payload[mask], mask)
    near = lax.ppermute(near, "grp", [(i, i ^ 1) for i in range(group_count)])
    curl, atm = pl.pallas_call(
        functools.partial(final_kernel, tile_count, back_count),
        out_shape=[shape((rows, cols), F32), shape((back_count, atm_flux.shape[1]), F32)],
        in_specs=[SMEM, SMEM] + [VMEM] * (5 + tile_count),
        out_specs=[VMEM] * 2,
        compiler_params=PARAMS,
        name="final",
    )(send_block, send_count, ocean_mask, stress_x, stress_y, near, far, *payload)
    return (heat, curl, atm)


def solution(mesh):
    placed = (
        P(None, ("grp", "tile")),
        P(("grp", "tile"), None, None),
        P(("grp", "tile"), None),
        P(("grp", "tile"), None, None),
        P(("grp", "tile"), None, None, None, None),
        P("grp", "tile"),
        P("grp", "tile"),
    )
    return jax.shard_map(
        per_device,
        mesh=mesh,
        in_specs=placed,
        out_specs=(P("grp", "tile"), P("grp", "tile"), P(None, ("grp", "tile"))),
        check_vma=False,
    )
```

time: 38.4 us -> 29.9 us (0.78)
  the two profiles are of different devices: /device:TPU:0 before, /device:TPU:3 now
where the time goes in v1:
time: 29.9 us; the launch traced here: 29.6 us
  starting transfers between devices  13.4 us (45%)
  waiting for transfers between devices  7.16 us (24%)
  local copies, waits for them, and re-layouts  4.57 us (15%)
  Pallas kernels  3.7 us (12%)
  between operations  0.7 us (2%)
    ppermute x6, starting transfers between devices, swap(): lax.ppermute(value, 'tile', [(i, i ^ mask) for i in range(tile_count)])  7.22 us
    unnamed x18, local copies, waits for them, and re-layouts  4.57 us
    ppermute x6, waiting for transfers between devices, swap(): lax.ppermute(value, 'tile', [(i, i ^ mask) for i in range(tile_count)])  4.39 us
    ppermute x1, starting transfers between devices, per_device(): near = lax.ppermute(near, 'grp', [(i, i ^ 1) for i in range(group_count)])  3.23 us
    ppermute x1, starting transfers between devices, per_device(): lax.ppermute(far, 'grp', [(i, i + 1 if i % 2 else i - 1) for i in range(1...  3 us
    ppermute x1, waiting for transfers between devices, per_device(): lax.ppermute(far, 'grp', [(i, i + 1 if i % 2 else i - 1) for i in range(1...  2.77 us
    pallas_call x1, Pallas kernels, per_device(): pl.pallas_call(functools.partial(middle_kernel, tile_count, field_count,...  1.77 us
    pallas_call x1, Pallas kernels, per_device(): pl.pallas_call(functools.partial(final_kernel, tile_count, back_count), o...  1.32 us
  transfers between devices with their start and end apart: 8, of which 3 were waited for; matrix products, arithmetic and copies ran while one was open for 0% of the time, Pallas kernels for 0%

profile of v1, /device:TPU:3, one launch (start us, length us, event | category | flops | bytes accessed | tf_op | source)
XLA Modules:
  0.0 29.6 jit_solution(5287680527160966103)
XLA Ops:
  0.6 0.0 copy-start.1
  0.6 0.0 copy-start.3
  0.6 0.8 %copy-done.3 = f32[6,1024]{1,0:T(8,128)S(1)} copy-done((f32[6,1024]{1,0:T(8,128)S(1)}, f32[6,1024]{1,0:T(8,128)}, u32[]{:S(2)}) %copy-start.3) | copy-done | bytes 24600
  1.4 0.0 copy-start.4
  1.4 0.7 %copy-done.4 = s32[1,4,4]{2,1,0:T(4,128)S(1)} copy-done((s32[1,4,4]{2,1,0:T(4,128)S(1)}, s32[1,4,4]{2,1,0:T(4,128)}, u32[]{:S(2)}) %copy-start.4) | copy-done | bytes 88
  2.1 0.0 copy-start.7
  2.1 0.7 %copy-done.7 = s32[1,4]{1,0:T(1,128)S(1)} copy-done((s32[1,4]{1,0:T(1,128)S(1)}, s32[1,4]{1,0:T(1,128)}, u32[]{:S(2)}) %copy-start.7) | copy-done | bytes 40
  2.7 0.6 %pack.1 = (f32[4,8,128]{2,1,0:T(8,128)S(1)}, f32[4,8,128]{2,1,0:T(8,128)S(1)}, f32[4,8,128]{2,1,0:T(8,128)S(1)}, f32[4,8,128]{2,1,0:T(8,128)S(1)}) custom-call(s32[1,4,4]{2,1,0:T(4,128)S(1)} %copy-done.4, s32[1,4]{1,0:T(1,128)S(1)} %copy-done.7, f32[6,1024]{1,0:T(8,128)S(1)} %copy-done.3), custom_call_target="tpu_custom_call" | custom-call | tf_op jit(solution)/shard_map/pack/pallas_call | solution.py:204
  3.4 1.4 %collective-permute-start = (f32[4,8,128]{2,1,0:T(8,128)S(1)}, f32[4,8,128]{2,1,0:T(8,128)S(1)}, u32[]{:S(2)}, u32[]{:S(2)}) collective-permute-start(f32[4,8,128]{2,1,0:T(8,128)S(1)} %get-tuple-element.19), channel_id=1, source_target_pairs={{0,1},{1,0},{2,3},{3,2},{4,5},{5,4},{6,7},{7,6},{8,9},{9,8},{10,11... | collective-permute-start | bytes 49160 | tf_op jit(solution)/shard_map/ppermute | solution.py:202
  4.7 0.0 copy-start.6
  4.7 2.3 %collective-permute-start.1 = (f32[4,8,128]{2,1,0:T(8,128)S(1)}, f32[4,8,128]{2,1,0:T(8,128)S(1)}, u32[]{:S(2)}, u32[]{:S(2)}) collective-permute-start(f32[4,8,128]{2,1,0:T(8,128)S(1)} %get-tuple-element.20), channel_id=1, source_target_pairs={{0,2},{1,3},{2,0},{3,1},{4,6},{5,7},{6,4},{7,5},{8,10},{9,11},{10,... | collective-permute-start | bytes 49160 | tf_op jit(solution)/shard_map/ppermute | solution.py:202
  7.0 0.0 collective-permute-start.2
  7.0 0.0 collective-permute-done.refs_1_
  7.0 1.3 %collective-permute-done.1.refs_2_ = f32[4,8,128]{2,1,0:T(8,128)S(1)} collective-permute-done((f32[4,8,128]{2,1,0:T(8,128)S(1)}, f32[4,8,128]{2,1,0:T(8,128)S(1)}, u32[]{:S(2)}, u32[]{:S(2)}) %collective-permute-start.1) | collective-permute-done | bytes 16416 | tf_op jit(solution)/shard_map/ppermute | solution.py:202
  8.4 3.0 %collective-permute-done.2.refs_3_ = f32[4,8,128]{2,1,0:T(8,128)S(1)} collective-permute-done((f32[4,8,128]{2,1,0:T(8,128)S(1)}, f32[4,8,128]{2,1,0:T(8,128)S(1)}, u32[]{:S(2)}, u32[]{:S(2)}) %collective-permute-start.2) | collective-permute-done | bytes 16416 | tf_op jit(solution)/shard_map/ppermute | solution.py:202
  11.4 0.0 copy-done.1
  11.4 0.0 copy-done.6
  11.4 0.0 copy-start
  11.4 1.0 %copy-done = bf16[1,4,4,128,128]{4,3,2,1,0:T(8,128)(2,1)S(1)} copy-done((bf16[1,4,4,128,128]{4,3,2,1,0:T(8,128)(2,1)S(1)}, bf16[1,4,4,128,128]{4,3,2,1,0:T(8,128)(2,1)}, u32[]{:S(2)}) %copy-start) | copy-done | bytes 524312
  12.5 0.0 copy-start.2
  12.5 0.8 %copy-done.2 = f32[32,256]{1,0:T(8,128)S(1)} copy-done((f32[32,256]{1,0:T(8,128)S(1)}, f32[32,256]{1,0:T(8,128)}, u32[]{:S(2)}) %copy-start.2) | copy-done | bytes 32792
  13.2 1.8 %middle.1 = (f32[32,256]{1,0:T(8,128)}, f32[32,256]{1,0:T(8,128)S(1)}, f32[32,256]{1,0:T(8,128)S(1)}, f32[2,128]{1,0:T(2,128)S(1)}, f32[2,128]{1,0:T(2,128)S(1)}...) custom-call(s32[1,4,4]{2,1,0:T(4,128)S(1)} %copy-done.6, ...), custom_call_target="tpu_custom_call" | custom-call | tf_op jit(solution)/shard_map/middle/pallas_call | solution.py:220
  15.0 0.2 collective-permute-start.7
  15.2 0.0 collective-permute-start.5
  15.2 3.4 %collective-permute-start.6 = (f32[16,128]{1,0:T(8,128)S(1)}, f32[16,128]{1,0:T(8,128)S(1)}, u32[]{:S(2)}, u32[]{:S(2)}) collective-permute-start(f32[16,128]{1,0:T(8,128)S(1)} %get-tuple-element.29), channel_id=1, source_target_pairs={{0,2},{1,3},{2,0},{3,1},{4,6},{5,7},{6,4},{7,5},{8,10},{9,11},{10,... | collective-permute-start | bytes 24584 | tf_op jit(solution)/shard_map/ppermute | solution.py:202
  18.6 3.2 %collective-permute-start.3 = (f32[2,128]{1,0:T(2,128)S(1)}, f32[2,128]{1,0:T(2,128)S(1)}, u32[]{:S(2)}, u32[]{:S(2)}) collective-permute-start(f32[2,128]{1,0:T(2,128)S(1)} %get-tuple-element.25), channel_id=1, source_target_pairs={{0,4},{4,0},{8,12},{12,8},{16,20},{20,16},{24,28},{28,24},{1,5},{5... | collective-permute-start | bytes 3080 | tf_op jit(solution)/shard_map/ppermute | solution.py:241
  21.8 3.0 %collective-permute-start.4 = (f32[2,128]{1,0:T(2,128)S(1)}, f32[2,128]{1,0:T(2,128)S(1)}, u32[]{:S(2)}, u32[]{:S(2)}) collective-permute-start(f32[2,128]{1,0:T(2,128)S(1)} %get-tuple-element.26), channel_id=1, source_target_pairs={{4,8},{8,4},{12,16},{16,12},{20,24},{24,20},{5,9},{9,5},{13,17},{1... | collective-permute-start | bytes 3080 | tf_op jit(solution)/shard_map/ppermute | solution.py:236
  24.8 0.0 collective-permute-done.3.near
  24.8 2.8 %collective-permute-done.4.far = f32[2,128]{1,0:T(2,128)S(1)} collective-permute-done((f32[2,128]{1,0:T(2,128)S(1)}, f32[2,128]{1,0:T(2,128)S(1)}, u32[]{:S(2)}, u32[]{:S(2)}) %collective-permute-start.4) | collective-permute-done | bytes 1056 | tf_op jit(solution)/shard_map/ppermute | solution.py:236
  27.6 0.0 collective-permute-done.6.refs_2_
  27.6 0.0 collective-permute-done.5.refs_1_
  27.6 0.0 collective-permute-done.7.refs_3_
  27.6 0.0 copy-start.5
  27.6 0.0 copy-start.8
  27.6 0.7 %copy-done.5 = s32[1,4,4]{2,1,0:T(4,128)S(1)} copy-done((s32[1,4,4]{2,1,0:T(4,128)S(1)}, s32[1,4,4]{2,1,0:T(4,128)}, u32[]{:S(2)}) %copy-start.5) | copy-done | bytes 88
  28.3 0.0 copy-done.8
  28.3 1.3 %final.1 = (f32[32,256]{1,0:T(8,128)}, f32[4,1024]{1,0:T(4,128)}) custom-call(s32[1,4,4]{2,1,0:T(4,128)S(1)} %copy-done.5, s32[1,4]{1,0:T(1,128)S(1)} %copy-done.8, s32[32,256]{1,0:T(8,128)S(1)} %copy-done.1, f32[32,256]{1,0:T(8,128)S(1)} %get-tuple-element.23.stress_x, f32[32,256]{1,0:T(8,128)S(1)} %get-tuple-element.24.stress_y, ...), custom_call_target="tpu_custom_call" | custom-call | tf_op jit(solution)/shard_map/final/pallas_call | solution.py:242
Async XLA Ops:
  0.6 10.8 %copy-start.1 = (s32[32,256]{1,0:T(8,128)S(1)}, s32[32,256]{1,0:T(8,128)}, u32[]{:S(2)}) copy-start(s32[32,256]{1,0:T(8,128)} %ocean_mask.3) | copy-start | bytes 98308
  0.6 0.8 %copy-start.3 = (f32[6,1024]{1,0:T(8,128)S(1)}, f32[6,1024]{1,0:T(8,128)}, u32[]{:S(2)}) copy-start(f32[6,1024]{1,0:T(8,128)} %atm_flux.1) | copy-start | bytes 73732
  1.4 0.7 %copy-start.4 = (s32[1,4,4]{2,1,0:T(4,128)S(1)}, s32[1,4,4]{2,1,0:T(4,128)}, u32[]{:S(2)}) copy-start(s32[1,4,4]{2,1,0:T(4,128)} %send_block.3) | copy-start | bytes 196
  2.1 0.7 %copy-start.7 = (s32[1,4]{1,0:T(1,128)S(1)}, s32[1,4]{1,0:T(1,128)}, u32[]{:S(2)}) copy-start(s32[1,4]{1,0:T(1,128)} %send_count.3) | copy-start | bytes 52
  3.4 3.7 %collective-permute-start = (f32[4,8,128]{2,1,0:T(8,128)S(1)}, f32[4,8,128]{2,1,0:T(8,128)S(1)}, u32[]{:S(2)}, u32[]{:S(2)}) collective-permute-start(f32[4,8,128]{2,1,0:T(8,128)S(1)} %get-tuple-element.19), channel_id=1, source_target_pairs={{0,1},{1,0},{2,3},{3,2},{4,5},{5,4},{6,7},{7,6},{8,9},{9,8},{10,11... | collective-permute-start | bytes 49160 | tf_op jit(solution)/shard_map/ppermute | solution.py:202
  4.7 6.7 %copy-start.6 = (s32[1,4,4]{2,1,0:T(4,128)S(1)}, s32[1,4,4]{2,1,0:T(4,128)}, u32[]{:S(2)}) copy-start(s32[1,4,4]{2,1,0:T(4,128)} %recv_block.1) | copy-start | bytes 196
  4.7 3.7 %collective-permute-start.1 = (f32[4,8,128]{2,1,0:T(8,128)S(1)}, f32[4,8,128]{2,1,0:T(8,128)S(1)}, u32[]{:S(2)}, u32[]{:S(2)}) collective-permute-start(f32[4,8,128]{2,1,0:T(8,128)S(1)} %get-tuple-element.20), channel_id=1, source_target_pairs={{0,2},{1,3},{2,0},{3,1},{4,6},{5,7},{6,4},{7,5},{8,10},{9,11},{10,... | collective-permute-start | bytes 49160 | tf_op jit(solution)/shard_map/ppermute | solution.py:202
  7.0 4.4 %collective-permute-start.2 = (f32[4,8,128]{2,1,0:T(8,128)S(1)}, f32[4,8,128]{2,1,0:T(8,128)S(1)}, u32[]{:S(2)}, u32[]{:S(2)}) collective-permute-start(f32[4,8,128]{2,1,0:T(8,128)S(1)} %get-tuple-element.21), channel_id=1, source_target_pairs={{0,3},{1,2},{2,1},{3,0},{4,7},{5,6},{6,5},{7,4},{8,11},{9,10},{10,... | collective-permute-start | bytes 49160 | tf_op jit(solution)/shard_map/ppermute | solution.py:202
  11.4 1.0 %copy-start = (bf16[1,4,4,128,128]{4,3,2,1,0:T(8,128)(2,1)S(1)}, bf16[1,4,4,128,128]{4,3,2,1,0:T(8,128)(2,1)}, u32[]{:S(2)}) copy-start(bf16[1,4,4,128,128]{4,3,2,1,0:T(8,128)(2,1)} %weight.1) | copy-start | bytes 1572868
  12.5 0.8 %copy-start.2 = (f32[32,256]{1,0:T(8,128)S(1)}, f32[32,256]{1,0:T(8,128)}, u32[]{:S(2)}) copy-start(f32[32,256]{1,0:T(8,128)} %sea_temp.1) | copy-start | bytes 98308
  15.0 12.6 %collective-permute-start.7 = (f32[26,128]{1,0:T(8,128)S(1)}, f32[26,128]{1,0:T(8,128)S(1)}, u32[]{:S(2)}, u32[]{:S(2)}) collective-permute-start(f32[26,128]{1,0:T(8,128)S(1)} %get-tuple-element.30), channel_id=1, source_target_pairs={{0,3},{1,2},{2,1},{3,0},{4,7},{5,6},{6,5},{7,4},{8,11},{9,10},{10,... | collective-permute-start | bytes 39944 | tf_op jit(solution)/shard_map/ppermute | solution.py:202
  15.2 12.4 %collective-permute-start.5 = (f32[24,128]{1,0:T(8,128)S(1)}, f32[24,128]{1,0:T(8,128)S(1)}, u32[]{:S(2)}, u32[]{:S(2)}) collective-permute-start(f32[24,128]{1,0:T(8,128)S(1)} %get-tuple-element.28), channel_id=1, source_target_pairs={{0,1},{1,0},{2,3},{3,2},{4,5},{5,4},{6,7},{7,6},{8,9},{9,8},{10,11... | collective-permute-start | bytes 36872 | tf_op jit(solution)/shard_map/ppermute | solution.py:202
  15.2 12.4 %collective-permute-start.6 = (f32[16,128]{1,0:T(8,128)S(1)}, f32[16,128]{1,0:T(8,128)S(1)}, u32[]{:S(2)}, u32[]{:S(2)}) collective-permute-start(f32[16,128]{1,0:T(8,128)S(1)} %get-tuple-element.29), channel_id=1, source_target_pairs={{0,2},{1,3},{2,0},{3,1},{4,6},{5,7},{6,4},{7,5},{8,10},{9,11},{10,... | collective-permute-start | bytes 24584 | tf_op jit(solution)/shard_map/ppermute | solution.py:202
  18.6 6.2 %collective-permute-start.3 = (f32[2,128]{1,0:T(2,128)S(1)}, f32[2,128]{1,0:T(2,128)S(1)}, u32[]{:S(2)}, u32[]{:S(2)}) collective-permute-start(f32[2,128]{1,0:T(2,128)S(1)} %get-tuple-element.25), channel_id=1, source_target_pairs={{0,4},{4,0},{8,12},{12,8},{16,20},{20,16},{24,28},{28,24},{1,5},{5... | collective-permute-start | bytes 3080 | tf_op jit(solution)/shard_map/ppermute | solution.py:241
  21.8 5.8 %collective-permute-start.4 = (f32[2,128]{1,0:T(2,128)S(1)}, f32[2,128]{1,0:T(2,128)S(1)}, u32[]{:S(2)}, u32[]{:S(2)}) collective-permute-start(f32[2,128]{1,0:T(2,128)S(1)} %get-tuple-element.26), channel_id=1, source_target_pairs={{4,8},{8,4},{12,16},{16,12},{20,24},{24,20},{5,9},{9,5},{13,17},{1... | collective-permute-start | bytes 3080 | tf_op jit(solution)/shard_map/ppermute | solution.py:236
  27.6 0.7 %copy-start.5 = (s32[1,4,4]{2,1,0:T(4,128)S(1)}, s32[1,4,4]{2,1,0:T(4,128)}, u32[]{:S(2)}) copy-start(s32[1,4,4]{2,1,0:T(4,128)} %send_block.3) | copy-start | bytes 196
  27.6 0.7 %copy-start.8 = (s32[1,4]{1,0:T(1,128)S(1)}, s32[1,4]{1,0:T(1,128)}, u32[]{:S(2)}) copy-start(s32[1,4]{1,0:T(1,128)} %send_count.3) | copy-start | bytes 52
